TPU v7x, 128 devices: a whole 4x4x4 slice. The times are simulated.
128 devices in a mesh: ex: 32 (over z, x, y_lo), feat: 4 (over y_hi, core).
Axes of the slice: x: 4, y: 4 (y_hi: 2, y_lo: 2; y = y_hi * 2 + y_lo), z: 4, core: 2. Of those that a mesh axis runs over, the one named last changes fastest.
Arguments:
- train_grads: bfloat16 [12288, 16384], P('ex', 'feat'), may hold values from -6 to 6
- projection: bfloat16 [16384, 4096], P('feat', 'ex'), may hold values from -0.046875 to 0.046875
- test_features: bfloat16 [1024, 4096], P('ex', 'feat'), may hold values from -0.09375 to 0.09375
- example_weights: float32 [12288], P('ex'), may hold values from 0.05 to 1
Outputs:
- scores: float32 [1024, 12288], P('feat', 'ex')
- projected: bfloat16 [12288, 4096], P('ex', 'feat')
All inputs are finite; a program needn't handle non-finite values.
Results may differ from a plain program's by a relative error of at most 0.0031.
Values may be sent and summed in bfloat16 or wider, within the bound.
A program may use at most 192 MiB of HBM per device.

v0:
```python
import jax
import jax.numpy as jnp
from jax import lax
from jax.sharding import Mesh
from jax.sharding import PartitionSpec as P

EX = ("ex_0", "ex_1", "ex_2")


def joined_along(pieces, dim):
    pieces = jnp.moveaxis(pieces, 0, dim)
    dims = pieces.shape
    return pieces.reshape(*dims[:dim], dims[dim] * dims[dim + 1], *dims[dim + 2 :])


def stacked_from(shard, axes, turns):
    pieces = shard[None]
    for k in turns:
        pieces = lax.all_gather(pieces, axes[k], axis=0, tiled=True)
    carried = [lax.axis_size(axes[k]) for k in reversed(turns)]
    pieces = pieces.reshape(*carried, *shard.shape)
    turned = sorted(range(len(turns)), key=lambda place: turns[len(turns) - 1 - place])
    return pieces.transpose(*turned, *range(len(turns), pieces.ndim)).reshape(-1, *shard.shape)


def gather_axes(shard, axes, turns, dim):
    return joined_along(stacked_from(shard, axes, turns), dim)


def in_blocks(shard, dim, length):
    before, after = (shard.shape[:dim], shard.shape[dim + 1 :])
    return jnp.moveaxis(shard.reshape(*before, length, -1, *after), dim, 0)


def summed_on_arrival(shard, axis, dim):
    length = lax.axis_size(axis)
    pieces = lax.all_to_all(in_blocks(shard, dim, length), axis, 0, 0, tiled=True)
    return jnp.sum(pieces, axis=0)


def local(train_grads, projection, test_features, example_weights):
    partial_value = jnp.dot(
        train_grads, gather_axes(projection, EX, (2, 0, 1), 1), preferred_element_type=jnp.float32
    )
    projected = lax.psum_scatter(partial_value, "feat", scatter_dimension=1, tiled=True).astype(
        jnp.bfloat16
    )
    partial_scores = lax.dot_general(
        lax.all_gather(test_features, EX, axis=0, tiled=True),
        projected,
        (((1,), (1,)), ((), ())),
        preferred_element_type=jnp.float32,
    )
    inner = summed_on_arrival(partial_scores, "feat", 0)
    return (inner * example_weights[None, :], projected)


def solution(mesh):
    finer = Mesh(
        mesh.devices.reshape(4, 4, 2, mesh.shape["feat"]), ("ex_0", "ex_1", "ex_2", "feat")
    )
    placed = (P(EX, "feat"), P("feat", EX), P(EX, "feat"), P(EX))
    return jax.shard_map(
        local,
        mesh=finer,
        in_specs=placed,
        out_specs=(P("feat", EX), P(EX, "feat")),
        check_vma=False,
    )
```

profile of v0, /device:TPU:1, one launch (start us, length us, event | category | flops | bytes accessed | tf_op | source)
XLA Modules:
  0.0 740.3 jit_solution(1886742789507018610)
XLA Ops:
  8.0 0.0 copy-start
  8.0 0.0 all-gather.12.cloned.1.call-start
  8.1 0.7 all-gather.12.cloned.1.call-update
  8.7 0.0 all-gather.6.cloned.1.call-start
  8.8 40.4 %all-gather.12.cloned.1.call-done = bf16[8192,128]{1,0:T(8,128)(2,1)} async-done(((bf16[4096,128]{1,0:T(8,128)(2,1)}), bf16[8192,128]{1,0:T(8,128)(2,1)}) %all-gather.12.cloned.1.call-update) | async-done | bytes 2097168 | tf_op jit(solution)/shard_map/all_gather | solution.py:19
  49.2 0.0 all-gather.6.cloned.1.call-update
  49.2 0.0 all-gather.8.cloned.1.call-start
  49.2 85.9 %all-gather.6.cloned.1.call-done = bf16[8,4096,128]{2,1,0:T(8,128)(2,1)} async-done(((bf16[2,4096,128]{2,1,0:T(8,128)(2,1)}), bf16[8,4096,128]{2,1,0:T(8,128)(2,1)}) %all-gather.6.cloned.1.call-update) | async-done | bytes 8388624 | tf_op jit(solution)/shard_map/all_gather | solution.py:19
  135.1 0.0 all-gather.8.cloned.1.call-update
  135.1 0.0 reduce-scatter.2.cloned.1.call-start
  135.2 296.2 %all-gather.8.cloned.1.call-done = bf16[32,4096,128]{2,1,0:T(8,128)(2,1)} async-done(((bf16[8,4096,128]{2,1,0:T(8,128)(2,1)}), bf16[32,4096,128]{2,1,0:T(8,128)(2,1)}) %all-gather.8.cloned.1.call-update) | async-done | bytes 33554448 | tf_op jit(solution)/shard_map/all_gather | solution.py:19
  431.4 22.9 %copy.9 = bf16[4,4,2,4096,128]{4,3,2,1,0:T(8,128)(2,1)} copy(bf16[4,4,2,4096,128]{4,3,2,0,1:T(8,128)(2,1)} %bitcast.18) | data formatting | bytes 67108864 | tf_op jit(solution)/shard_map/transpose | solution.py:23
  454.3 41.1 %copy.10 = bf16[4096,32,128]{0,2,1:T(8,128)(2,1)} copy(bf16[4096,32,128]{2,0,1:T(8,128)(2,1)} %bitcast.17) | data formatting | bytes 67108864 | tf_op jit(solution)/shard_map/transpose | solution.py:11
  495.4 0.0 copy-done
  495.4 19.8 %fusion = f32[384,4096]{1,0:T(8,128)} fusion(bf16[384,4096]{1,0:T(8,128)(2,1)S(1)} %copy-done, bf16[4096,4096]{0,1:T(8,128)(2,1)} %bitcast.19), kind=kOutput, calls=%fused_computation.2 | convolution fusion | flops 12884901888 | bytes 42991616 | tf_op jit(solution)/shard_map/dot_general | solution.py:42
  515.2 0.0 reduce-scatter.2.cloned.1.call-update
  515.3 0.0 all-gather.10.cloned.1.call-start
  515.3 0.5 all-gather.10.cloned.1.call-update
  515.8 66.9 %reduce-scatter.2.cloned.1.call-done = f32[384,1024]{1,0:T(8,128)} async-done(((f32[384,4096]{1,0:T(8,128)}), f32[384,1024]{1,0:T(8,128)}) %reduce-scatter.2.cloned.1.call-update) | async-done | bytes 1572880 | tf_op jit(solution)/shard_map/reduce_scatter | solution.py:45
  582.7 1.5 convert_element_type.3
  584.3 0.0 copy-start.2
  584.3 94.7 %all-gather.10.cloned.1.call-done = bf16[1024,1024]{1,0:T(8,128)(2,1)} async-done(((bf16[32,1024]{1,0:T(8,128)(2,1)}), bf16[1024,1024]{1,0:T(8,128)(2,1)}) %all-gather.10.cloned.1.call-update) | async-done | bytes 2097168 | tf_op jit(solution)/shard_map/all_gather | solution.py:49
  679.0 2.6 fusion.1
  681.6 0.0 copy-done.2
  681.7 0.1 copy.17
  681.8 0.0 copy-start.3
  681.8 0.0 copy-start.1
  681.8 47.0 %all_to_all.5 = f32[4,256,384]{1,2,0:T(8,128)} all-to-all(f32[4,256,384]{1,2,0:T(8,128)S(1)} %bitcast.20), channel_id=1, replica_groups=mesh['ex_0'=4,'ex_1'=4,'ex_2'=2,'feat'=4] {'feat'}, dimensions={0} | all-to-all | bytes 3145728 | tf_op jit(solution)/shard_map/all_to_all | solution.py:37
  728.8 2.3 reduce_sum.9
  731.1 0.0 copy-done.3
  731.1 1.1 broadcast_multiply_fusion
  732.2 0.9 copy.13
  (1 shorter events, 0.0 us)
Async XLA Ops:
  8.0 487.4 %copy-start = (bf16[384,4096]{1,0:T(8,128)(2,1)S(1)}, bf16[384,4096]{1,0:T(8,128)(2,1)}, u32[]{:S(2)}) copy-start(bf16[384,4096]{1,0:T(8,128)(2,1)} %param.4) | copy-start | bytes 9437188
  8.0 41.1 %all-gather.12.cloned.1.call-start = ((), (), s32[]{:S(2)}) async-start(), calls=%async_computation.6 | async-start | bytes 3145728 | tf_op jit(solution)/shard_map/all_gather | solution.py:19
  8.7 126.4 %all-gather.6.cloned.1.call-start = ((), (), s32[]{:S(2)}) async-start(), calls=%async_computation.2 | async-start | bytes 10485760 | tf_op jit(solution)/shard_map/all_gather | solution.py:19
  49.2 382.2 %all-gather.8.cloned.1.call-start = ((), (), s32[]{:S(2)}) async-start(), calls=%async_computation.3 | async-start | bytes 41943040 | tf_op jit(solution)/shard_map/all_gather | solution.py:19
  135.1 447.6 %reduce-scatter.2.cloned.1.call-start = ((), (), s32[]{:S(2)}) async-start(), calls=%async_computation.4 | async-start | bytes 7864320 | tf_op jit(solution)/shard_map/reduce_scatter | solution.py:45
  515.3 163.8 %all-gather.10.cloned.1.call-start = ((), (), s32[]{:S(2)}) async-start(), calls=%async_computation.5 | async-start | bytes 2162688 | tf_op jit(solution)/shard_map/all_gather | solution.py:49
  584.3 97.4 %copy-start.2 = (bf16[384,1024]{1,0:T(8,128)(2,1)}, bf16[384,1024]{1,0:T(8,128)(2,1)S(1)}, u32[]{:S(2)}) copy-start(bf16[384,1024]{1,0:T(8,128)(2,1)S(1)} %convert_element_type.3) | copy-start | bytes 2359300
  681.8 49.3 %copy-start.3 = (f32[384]{0:T(512)S(1)}, f32[384]{0:T(512)}, u32[]{:S(2)}) copy-start(f32[384]{0:T(512)} %param.7) | copy-start | bytes 4612
  681.8 51.3 %copy-start.1 = (bf16[384,4096]{1,0:T(8,128)(2,1)S(1)}, bf16[384,4096]{1,0:T(8,128)(2,1)}, u32[]{:S(2)}) copy-start(bf16[384,4096]{1,0:T(8,128)(2,1)} %param.4) | copy-start | bytes 9437188
Sparse Core Ops, SparseCore 0:
  10.5 38.6 all-gather.11
  50.8 84.2 all-gather.5
  136.8 294.5 all-gather.7
  515.4 67.3 reduce-scatter.1
Sparse Core Ops, SparseCore 1:
  517.4 161.6 all-gather.9
where the time goes:
time: 742 us; the launch traced here: 740 us
  waiting for transfers between devices  585 us (79%)
  local copies, waits for them, and re-layouts  65.1 us (9%)
  blocking collectives  47 us (6%)
  matrix products  22.4 us (3%)
  between operations  15.3 us (2%)
    all_gather x3, waiting for transfers between devices, stacked_from(): pieces = lax.all_gather(pieces, axes[k], axis=0, tiled=True)  422 us
    all_gather x1, waiting for transfers between devices, local(): lax.all_gather(test_features, EX, axis=0, tiled=True)  94.7 us
    reduce_scatter x1, waiting for transfers between devices, local(): lax.psum_scatter(partial_value, 'feat', scatter_dimension=1, tiled=True)  66.9 us
    all_to_all x1, blocking collectives, summed_on_arrival(): lax.all_to_all(in_blocks(shard, dim, length), axis, 0, 0, tiled=True)  47 us
    transpose x1, local copies, waits for them, and re-layouts, joined_along(): pieces = jnp.moveaxis(pieces, 0, dim)  41.1 us
    transpose x1, local copies, waits for them, and re-layouts, stacked_from(): pieces.transpose(*turned, *range(len(turns), pieces.ndim))  22.9 us
    dot_general x1, matrix products, local(): jnp.dot(train_grads, gather_axes(projection, EX, (2, 0, 1), 1), preferred...  19.8 us
  transfers between devices with their start and end apart: 5, of which 5 were waited for; matrix products, arithmetic and copies ran while one was open for 0% of the time, Pallas kernels for 0%

commit v1 on v0

--- a/solution.py
+++ b/solution.py
@@ -5,6 +5,13 @@
 from jax.sharding import PartitionSpec as P
 
 EX = ("ex_0", "ex_1", "ex_2")
+
+
+def all_by_exchange(x, axis, along):
+    n_dev = lax.axis_size(axis)
+    shards = jnp.stack([x for _ in range(n_dev)])
+    shards = lax.all_to_all(shards, axis, split_axis=0, concat_axis=0)
+    return jnp.concatenate(shards, axis=along)
 
 
 def joined_along(pieces, dim):
@@ -16,7 +23,7 @@
 def stacked_from(shard, axes, turns):
     pieces = shard[None]
     for k in turns:
-        pieces = lax.all_gather(pieces, axes[k], axis=0, tiled=True)
+        pieces = all_by_exchange(pieces, axes[k], 0)
     carried = [lax.axis_size(axes[k]) for k in reversed(turns)]
     pieces = pieces.reshape(*carried, *shard.shape)
     turned = sorted(range(len(turns)), key=lambda place: turns[len(turns) - 1 - place])

time: 742 us -> 846 us (1.14)
  blocking collectives: 47 us -> 503 us
  waiting for transfers between devices: 585 us -> 179 us
  starting transfers between devices: 0.2 us -> 27.6 us
  local copies, waits for them, and re-layouts: 65.1 us -> 84.2 us
    all_to_all x1 -> x3, blocking collectives: 47 us -> 503 us  [all_by_exchange(): shards = lax.all_to_all(shards, axis, split_axis=0, concat_axis=0)]
    all_gather x3 -> x0, waiting for transfers between devices: 422 us -> none  [stacked_from(): pieces = lax.all_gather(pieces, axes[k], axis=0, tiled=True)]
    all_to_all x0 -> x1, starting transfers between devices: none -> 27.5 us  [summed_on_arrival(): lax.all_to_all(in_blocks(shard, dim, length), axis, 0, 0, tiled=True)]
    all_to_all x0 -> x1, waiting for transfers between devices: none -> 18.4 us  [summed_on_arrival(): lax.all_to_all(in_blocks(shard, dim, length), axis, 0, 0, tiled=True)]
    another operation x0 -> x2, local copies, waits for them, and re-layouts: none -> 15.3 us  [all_by_exchange(): shards = jnp.stack([x for _ in range(n_dev)])]
  transfers between devices with their start and end apart: 5 -> 3, of which waited for: 5 -> 3; matrix products, arithmetic and copies ran while one was open for 0% -> 1% of each run, Pallas kernels for 0% -> 0%
where the time goes in v1:
time: 846 us; the launch traced here: 844 us
  blocking collectives  503 us (59%)
  waiting for transfers between devices  179 us (21%)
  local copies, waits for them, and re-layouts  84.2 us (10%)
  starting transfers between devices  27.6 us (3%)
  matrix products  26.5 us (3%)
  between operations  15.5 us (2%)
    all_to_all x3, blocking collectives, all_by_exchange(): shards = lax.all_to_all(shards, axis, split_axis=0, concat_axis=0)  503 us
    all_gather x1, waiting for transfers between devices, local(): lax.all_gather(test_features, EX, axis=0, tiled=True)  93.4 us
    reduce_scatter x1, waiting for transfers between devices, local(): lax.psum_scatter(partial_value, 'feat', scatter_dimension=1, tiled=True)  67.2 us
    transpose x1, local copies, waits for them, and re-layouts, joined_along(): pieces = jnp.moveaxis(pieces, 0, dim)  41.5 us
    all_to_all x1, starting transfers between devices, summed_on_arrival(): lax.all_to_all(in_blocks(shard, dim, length), axis, 0, 0, tiled=True)  27.5 us
    dot_general x1, matrix products, local(): jnp.dot(train_grads, gather_axes(projection, EX, (2, 0, 1), 1), preferred...  23.6 us
    transpose x1, local copies, waits for them, and re-layouts, stacked_from(): pieces.transpose(*turned, *range(len(turns), pieces.ndim))  22.8 us
    all_to_all x1, waiting for transfers between devices, summed_on_arrival(): lax.all_to_all(in_blocks(shard, dim, length), axis, 0, 0, tiled=True)  18.4 us
  transfers between devices with their start and end apart: 3, of which 3 were waited for; matrix products, arithmetic and copies ran while one was open for 1% of the time, Pallas kernels for 0%

profile of v1, /device:TPU:1, one launch (start us, length us, event | category | flops | bytes accessed | tf_op | source)
XLA Modules:
  0.0 843.9 jit_solution(3687870152594547294)
XLA Ops:
  8.0 0.0 copy-start
  8.0 0.0 reduce-scatter.2.cloned.1.call-start
  8.1 1.9 pad_maximum_fusion
  9.9 27.2 %all_to_all.20 = bf16[2,1,4096,128]{3,2,1,0:T(8,128)(2,1)S(1)} all-to-all(bf16[2,1,4096,128]{3,2,1,0:T(8,128)(2,1)S(1)} %pad_maximum_fusion), channel_id=1, replica_groups=mesh['ex_0'=4,'ex_1'=4,'ex_2'=2,'feat'=4] {'ex_2'}, dimensions={0} | all-to-all | bytes 4194304 | tf_op jit(solution)/shard_map/all_to_all | solution.py:13
  37.1 4.3 stack.10
  41.4 97.3 %all_to_all.21 = bf16[4,2,4096,128]{3,2,1,0:T(8,128)(2,1)S(1)} all-to-all(bf16[4,2,4096,128]{3,2,1,0:T(8,128)(2,1)} %stack.10), channel_id=1, replica_groups=mesh['ex_0'=4,'ex_1'=4,'ex_2'=2,'feat'=4] {'ex_0'}, dimensions={0} | all-to-all | bytes 16777216 | tf_op jit(solution)/shard_map/all_to_all | solution.py:13
  138.7 11.1 %stack.11 = bf16[4,8,4096,128]{3,2,1,0:T(8,128)(2,1)} broadcast(bf16[8,4096,128]{2,1,0:T(8,128)(2,1)S(1)} %bitcast.23), dimensions={1,2,3} | broadcast | bytes 41943040 | tf_op jit(solution)/shard_map/stack | solution.py:12
  149.8 378.6 %all_to_all.22 = bf16[4,8,4096,128]{3,2,1,0:T(8,128)(2,1)} all-to-all(bf16[4,8,4096,128]{3,2,1,0:T(8,128)(2,1)} %stack.11), channel_id=1, replica_groups=mesh['ex_0'=4,'ex_1'=4,'ex_2'=2,'feat'=4] {'ex_1'}, dimensions={0} | all-to-all | bytes 67108864 | tf_op jit(solution)/shard_map/all_to_all | solution.py:13
  528.4 22.8 %copy.12 = bf16[4,4,2,4096,128]{4,3,2,1,0:T(8,128)(2,1)} copy(bf16[4,4,2,4096,128]{4,3,2,0,1:T(8,128)(2,1)} %bitcast.21) | data formatting | bytes 67108864 | tf_op jit(solution)/shard_map/transpose | solution.py:30
  551.2 41.5 %copy.13 = bf16[4096,32,128]{0,2,1:T(8,128)(2,1)} copy(bf16[4096,32,128]{2,0,1:T(8,128)(2,1)} %bitcast.22) | data formatting | bytes 67108864 | tf_op jit(solution)/shard_map/transpose | solution.py:18
  592.7 0.0 copy-done
  592.7 23.6 %convolution_bitcast_fusion = f32[384,4096]{0,1:T(8,128)} fusion(bf16[4096,4096]{0,1:T(8,128)(2,1)} %bitcast.24, bf16[384,4096]{1,0:T(8,128)(2,1)S(1)} %copy-done), kind=kOutput, calls=%fused_computation | convolution fusion | flops 12884901888 | bytes 42991616 | tf_op jit(solution)/shard_map/dot_general | solution.py:49
  616.4 0.0 reduce-scatter.2.cloned.1.call-update
  616.4 0.0 all-gather.2.cloned.1.call-start
  616.4 0.5 all-gather.2.cloned.1.call-update
  617.0 67.2 %reduce-scatter.2.cloned.1.call-done = f32[384,1024]{0,1:T(8,128)} async-done(((f32[384,4096]{0,1:T(8,128)}), f32[384,1024]{0,1:T(8,128)}) %reduce-scatter.2.cloned.1.call-update) | async-done | bytes 1572880 | tf_op jit(solution)/shard_map/reduce_scatter | solution.py:52
  684.1 2.4 convert_element_type.3
  686.5 93.4 %all-gather.2.cloned.1.call-done = bf16[1024,1024]{1,0:T(8,128)(2,1)} async-done(((bf16[32,1024]{1,0:T(8,128)(2,1)}), bf16[1024,1024]{1,0:T(8,128)(2,1)}) %all-gather.2.cloned.1.call-update) | async-done | bytes 2097168 | tf_op jit(solution)/shard_map/all_gather | solution.py:56
  779.8 2.9 fusion
  782.7 1.3 copy.21
  784.0 0.0 copy-start.1
  784.0 27.5 %all-to-all-start.3 = ((f32[4,256,384]{1,2,0:T(8,128)}), f32[4,256,384]{1,2,0:T(8,128)}, u32[]{:S(2)}, u32[]{:S(2)}) async-start(f32[4,256,384]{1,2,0:T(8,128)} %bitcast.26), calls=%async_computation.4 | async-start | bytes 3145728 | tf_op jit(solution)/shard_map/all_to_all | solution.py:44
  811.5 2.3 copy.17
  813.8 18.4 %all-to-all-done.3 = f32[4,256,384]{1,2,0:T(8,128)} async-done(((f32[4,256,384]{1,2,0:T(8,128)}), f32[4,256,384]{1,2,0:T(8,128)}, u32[]{:S(2)}, u32[]{:S(2)}) %all-to-all-start.3) | async-done | bytes 1572896 | tf_op jit(solution)/shard_map/all_to_all | solution.py:44
  832.2 2.3 reduce_sum.9
  834.5 0.0 copy-done.1
  834.5 1.1 broadcast_multiply_fusion
  835.6 0.9 copy.16
Async XLA Ops:
  8.0 584.7 %copy-start = (bf16[384,4096]{1,0:T(8,128)(2,1)S(1)}, bf16[384,4096]{1,0:T(8,128)(2,1)}, u32[]{:S(2)}) copy-start(bf16[384,4096]{1,0:T(8,128)(2,1)} %param.4) | copy-start | bytes 9437188
  8.0 676.1 %reduce-scatter.2.cloned.1.call-start = ((), (), s32[]{:S(2)}) async-start(), calls=%async_computation.5 | async-start | bytes 7864320 | tf_op jit(solution)/shard_map/reduce_scatter | solution.py:52
  616.4 163.5 %all-gather.2.cloned.1.call-start = ((), (), s32[]{:S(2)}) async-start(), calls=%async_computation.6 | async-start | bytes 2162688 | tf_op jit(solution)/shard_map/all_gather | solution.py:56
  784.0 50.5 %copy-start.1 = (f32[384]{0:T(512)S(1)}, f32[384]{0:T(512)}, u32[]{:S(2)}) copy-start(f32[384]{0:T(512)} %param.7) | copy-start | bytes 4612
  784.0 48.2 %all-to-all-start.3 = ((f32[4,256,384]{1,2,0:T(8,128)}), f32[4,256,384]{1,2,0:T(8,128)}, u32[]{:S(2)}, u32[]{:S(2)}) async-start(f32[4,256,384]{1,2,0:T(8,128)} %bitcast.26), calls=%async_computation.4 | async-start | bytes 3145728 | tf_op jit(solution)/shard_map/all_to_all | solution.py:44
Sparse Core Ops, SparseCore 0:
  616.5 67.5 reduce-scatter.1
Sparse Core Ops, SparseCore 1:
  618.5 161.3 all-gather.1
